TPU v7x, 32 devices: a whole 2x2x4 slice. The times are simulated.
32 devices in a mesh: att: 8 (over z, y), emb: 4 (over x, core).
Axes of the slice: x: 2, y: 2, z: 4, core: 2. Of those that a mesh axis runs over, the one named last changes fastest.
Arguments:
- w_qkv: float32 [4, 3, 2048, 2048], P(None, None, 'emb', 'att')
- w_out: float32 [4, 2048, 2048], P(None, 'att', 'emb')
- x_in: bfloat16 [4, 6144, 2048], P(None, None, 'emb')
- dy_qkv: bfloat16 [4, 3, 6144, 2048], P(None, None, None, 'att')
- x_attn: bfloat16 [4, 6144, 2048], P(None, None, 'att')
- dy_out: bfloat16 [4, 6144, 2048], P(None, None, 'emb')
- r_qkv: float32 [4, 3, 2048], P(None, None, 'emb')
- c_qkv: float32 [4, 3, 2048], P(None, None, 'att')
- r_out: float32 [4, 2048], P(None, 'att')
- c_out: float32 [4, 2048], P(None, 'emb')
- hyper_params: float32 [3], replicated
Outputs:
- output 1: float32 [4, 3, 2048, 2048], P(None, None, 'emb', 'att')
- output 2: float32 [4, 2048, 2048], P(None, 'att', 'emb')
- output 3: float32 [4, 3, 2048], P(None, None, 'emb')
- output 4: float32 [4, 3, 2048], P(None, None, 'att')
- output 5: float32 [4, 2048], P(None, 'att')
- output 6: float32 [4, 2048], P(None, 'emb')
All inputs are finite; a program needn't handle non-finite values.
Results may differ from a plain program's by a relative error of at most 0.001.
Values are sent between devices in bfloat16 or wider.
A program may use at most 1 GiB of HBM per device.

v0:
```python
import jax
import jax.numpy as jnp
from jax import lax
from jax.sharding import PartitionSpec as P

EPS_SQUARE = 1e-30
EPS_SCALE = 1e-3


def factored_step(w_grad, weight, row_old, col_old, hyper_params, m_axis, n_axis, m_total, n_total):
    beta_two = hyper_params[0]
    rel_step = hyper_params[1]
    clip_limit = hyper_params[2]
    q_sq = w_grad * w_grad + EPS_SQUARE
    row_part = jnp.sum(q_sq, axis=2)
    col_part = jnp.sum(q_sq, axis=1)
    lead_flag = (lax.axis_index(n_axis) == 0).astype(jnp.float32)
    scalar_part = jnp.stack(
        [jnp.sum(col_part, axis=1), jnp.sum(weight * weight, axis=(1, 2)), lead_flag * jnp.sum(row_old, axis=1)],
        axis=1,
    )
    row_sum = lax.psum(row_part, n_axis)
    col_sum = lax.psum(col_part, m_axis)
    scalar_sum = lax.psum(scalar_part, (m_axis, n_axis))
    n_elems = m_total * n_total
    row_new = beta_two * row_old + (1.0 - beta_two) * (row_sum / n_total)
    col_new = beta_two * col_old + (1.0 - beta_two) * (col_sum / m_total)
    mean_row = beta_two * scalar_sum[:, 2] / m_total + (1.0 - beta_two) * scalar_sum[:, 0] / n_elems
    row_factor = lax.rsqrt(row_new / mean_row[:, None])
    col_factor = lax.rsqrt(col_new)
    update = w_grad * row_factor[:, :, None] * col_factor[:, None, :]
    u_sum = lax.psum(jnp.sum(update * update, axis=(1, 2)), (m_axis, n_axis))
    rms_u = jnp.sqrt(u_sum / n_elems)
    rms_w = jnp.sqrt(scalar_sum[:, 1] / n_elems)
    step_size = rel_step * jnp.maximum(EPS_SCALE, rms_w) / jnp.maximum(1.0, rms_u / clip_limit)
    return weight - step_size[:, None, None] * update, row_new, col_new


def solution(mesh):
    emb_size = mesh.shape["emb"]
    att_size = mesh.shape["att"]
    in_specs = (
        P(None, None, "emb", "att"),
        P(None, "att", "emb"),
        P(None, None, "emb"),
        P(None, None, None, "att"),
        P(None, None, "att"),
        P(None, None, "emb"),
        P(None, None, "emb"),
        P(None, None, "att"),
        P(None, "att"),
        P(None, "emb"),
        P(),
    )
    out_specs = (
        P(None, None, "emb", "att"),
        P(None, "att", "emb"),
        P(None, None, "emb"),
        P(None, None, "att"),
        P(None, "att"),
        P(None, "emb"),
    )

    def local_run(w_qkv, w_out, x_in, dy_qkv, x_attn, dy_out, r_qkv, c_qkv, r_out, c_out, hyper_params):
        d_model = x_in.shape[2] * emb_size
        inner_dim = x_attn.shape[2] * att_size
        per_layer = []
        for layer_idx in range(w_qkv.shape[0]):
            g_qkv = jnp.einsum("td,ktn->kdn", x_in[layer_idx], dy_qkv[layer_idx], preferred_element_type=jnp.float32)
            new_qkv = factored_step(
                g_qkv, w_qkv[layer_idx], r_qkv[layer_idx], c_qkv[layer_idx], hyper_params, "emb", "att", d_model, inner_dim
            )
            g_out = jnp.einsum("ti,td->id", x_attn[layer_idx], dy_out[layer_idx], preferred_element_type=jnp.float32)
            new_out = factored_step(
                g_out[None], w_out[layer_idx][None], r_out[layer_idx][None], c_out[layer_idx][None],
                hyper_params, "att", "emb", inner_dim, d_model
            )
            per_layer.append((new_qkv[0], new_out[0][0], new_qkv[1], new_qkv[2], new_out[1][0], new_out[2][0]))
        return tuple(jnp.stack([layer_out[out_slot] for layer_out in per_layer]) for out_slot in range(6))

    return jax.shard_map(local_run, mesh=mesh, in_specs=in_specs, out_specs=out_specs, check_vma=False)
```

profile of v0, /device:TPU:0, one launch (start us, length us, event | category | flops | bytes accessed | tf_op | source)
XLA Modules:
  0.0 363.8 jit_solution(10881063504892395882)
XLA Ops:
  0.7 1.4 fusion.110
  2.7 1.5 slice_reduce_fusion.3
  6.7 2.4 multiply_reduce_fusion.11
  9.3 6.4 %fusion.64 = (f32[256]{0:T(256)S(1)}, f32[512]{0:T(512)S(1)}, f32[]{:T(128)}, f32[256,512]{1,0:T(8,128)S(1)}) fusion(bf16[4,6144,512]{2,1,0:T(8,128)(2,1)} %param.16, bf16[4,6144,256]{2,1,0:T(8,128)(2,1)} %param.15), kind=kOutput, calls=%fused_computation.106 | convolution fusion | flops 1611267328 | bytes 9964548 | tf_op jit(solution)/shard_map/ti,td->id/dot_general | solution.py:73
  15.7 2.4 pad_maximum_fusion.11
  18.1 6.5 %fusion.61 = (f32[256]{0:T(256)S(1)}, f32[512]{0:T(512)S(1)}, f32[]{:T(128)}, f32[256,512]{1,0:T(8,128)S(1)}) fusion(bf16[4,6144,512]{2,1,0:T(8,128)(2,1)} %param.16, bf16[4,6144,256]{2,1,0:T(8,128)(2,1)} %param.15), kind=kOutput, calls=%fused_computation.103 | convolution fusion | flops 1611267328 | bytes 9964548 | tf_op jit(solution)/shard_map/ti,td->id/dot_general | solution.py:73
  24.6 1.4 pad_maximum_fusion.10
  25.9 5.1 %fusion.70 = (f32[256]{0:T(256)S(1)}, f32[512]{0:T(512)S(1)}, f32[]{:T(128)}, f32[256,512]{1,0:T(8,128)}) fusion(bf16[4,6144,512]{2,1,0:T(8,128)(2,1)S(1)} %copy-done.15, bf16[4,6144,256]{2,1,0:T(8,128)(2,1)} %param.15), kind=kOutput, calls=%fused_computation.112 | convolution fusion | flops 1611267328 | bytes 9964548 | tf_op jit(solution)/shard_map/ti,td->id/dot_general | solution.py:73
  31.0 1.4 pad_maximum_fusion.13
  32.4 5.1 %fusion.67 = (f32[256]{0:T(256)S(1)}, f32[512]{0:T(512)S(1)}, f32[]{:T(128)}, f32[256,512]{1,0:T(8,128)}) fusion(bf16[4,6144,512]{2,1,0:T(8,128)(2,1)S(1)} %copy-done.15, bf16[4,6144,256]{2,1,0:T(8,128)(2,1)} %param.15), kind=kOutput, calls=%fused_computation.109 | convolution fusion | flops 1611267328 | bytes 9964548 | tf_op jit(solution)/shard_map/ti,td->id/dot_general | solution.py:73
  37.5 1.3 pad_maximum_fusion.12
  38.8 42.1 %all-reduce.1 = (f32[1,3]{1,0:T(1,128)S(1)}, f32[1,3]{1,0:T(1,128)S(1)}, f32[1,3]{1,0:T(1,128)S(1)}, f32[1,3]{1,0:T(1,128)S(1)}) all-reduce(f32[1,3]{1,0:T(1,128)S(1)} %pad_maximum_fusion.13, f32[1,3]{1,0:T(1,128)S(1)} %pad_maximum_fusion.12, f32[1,3]{1,0:T(1,128)S(1)} %pad_maximum_fusion.11, ...), channel_id=1, replica_groups=mesh['att'=8,'emb'=4] {'att','emb'}, use_global_device_ids=true, to_apply=%region_73.0 | all-reduce | flops 12 | bytes 96 | tf_op jit(solution)/shard_map/psum | solution.py:24
  80.9 0.7 fusion.108
  87.8 0.7 fusion.106
  94.7 11.0 %fusion.52 = (f32[3,512]{1,0:T(4,128)S(1)}, f32[3,256]{1,0:T(4,128)S(1)}, f32[3]{0:T(128)S(1)}, f32[3,256,512]{2,1,0:T(8,128)}) fusion(bf16[4,6144,512]{2,1,0:T(8,128)(2,1)} %param.13, bf16[4,3,6144,256]{3,2,1,0:T(8,128)(2,1)} %param.14), kind=kOutput, calls=%fused_computation.74 | convolution fusion | flops 4833802240 | bytes 17310732 | tf_op jit(solution)/shard_map/td,ktn->kdn/dot_general | solution.py:69
  105.7 11.0 %fusion.49 = (f32[3,512]{1,0:T(4,128)S(1)}, f32[3,256]{1,0:T(4,128)S(1)}, f32[3]{0:T(128)S(1)}, f32[3,256,512]{2,1,0:T(8,128)}) fusion(bf16[4,6144,512]{2,1,0:T(8,128)(2,1)} %param.13, bf16[4,3,6144,256]{3,2,1,0:T(8,128)(2,1)} %param.14), kind=kOutput, calls=%fused_computation.71 | convolution fusion | flops 4833802240 | bytes 17310732 | tf_op jit(solution)/shard_map/td,ktn->kdn/dot_general | solution.py:69
  116.8 11.0 %fusion.58 = (f32[3,512]{1,0:T(4,128)S(1)}, f32[3,256]{1,0:T(4,128)S(1)}, f32[3]{0:T(128)S(1)}, f32[3,256,512]{2,1,0:T(8,128)}) fusion(bf16[4,6144,512]{2,1,0:T(8,128)(2,1)} %param.13, bf16[4,3,6144,256]{3,2,1,0:T(8,128)(2,1)} %param.14), kind=kOutput, calls=%fused_computation.80 | convolution fusion | flops 4833802240 | bytes 17310732 | tf_op jit(solution)/shard_map/td,ktn->kdn/dot_general | solution.py:69
  127.8 11.2 %fusion.55 = (f32[3,512]{1,0:T(4,128)S(1)}, f32[3,256]{1,0:T(4,128)S(1)}, f32[3]{0:T(128)S(1)}, f32[3,256,512]{2,1,0:T(8,128)}) fusion(bf16[4,6144,512]{2,1,0:T(8,128)(2,1)} %param.13, bf16[4,3,6144,256]{3,2,1,0:T(8,128)(2,1)} %param.14), kind=kOutput, calls=%fused_computation.77 | convolution fusion | flops 4833802240 | bytes 17310732 | tf_op jit(solution)/shard_map/td,ktn->kdn/dot_general | solution.py:69
  139.0 37.4 %all-reduce.4 = (f32[3,512]{1,0:T(4,128)S(1)}, f32[3,512]{1,0:T(4,128)S(1)}, f32[3,512]{1,0:T(4,128)S(1)}, f32[3,512]{1,0:T(4,128)S(1)}, f32[1,512]{1,0:T(1,128)...) all-reduce(f32[3,512]{1,0:T(4,128)S(1)} %get-tuple-element.31, ...), channel_id=1, replica_groups=mesh['att'=8,'emb'=4] {'att'}, use_global_device_ids=true, to_apply=%region_35.0 | all-reduce | flops 8192 | bytes 65536 | tf_op jit(solution)/shard_map/psum | solution.py:22
  176.3 10.4 %all-reduce.5 = (f32[3,256]{1,0:T(4,128)S(1)}, f32[3,256]{1,0:T(4,128)S(1)}, f32[3,256]{1,0:T(4,128)S(1)}, f32[3,256]{1,0:T(4,128)S(1)}, f32[1,256]{1,0:T(1,128)...) all-reduce(f32[3,256]{1,0:T(4,128)S(1)} %get-tuple-element.32, ...), channel_id=1, replica_groups=mesh['att'=8,'emb'=4] {'emb'}, use_global_device_ids=true, to_apply=%region_37.0 | all-reduce | flops 4096 | bytes 32768 | tf_op jit(solution)/shard_map/psum | solution.py:23
  186.7 0.7 fusion.96
  187.4 0.7 divide_rsqrt_fusion.7
  188.0 0.6 pad_maximum_fusion.5
  188.6 0.7 fusion.92
  189.3 0.6 copy.58
  189.9 0.7 fusion.100
  190.6 1.9 multiply_reduce_fusion.4
  192.4 1.9 multiply_reduce_fusion.6
  194.4 0.8 multiply_reduce_fusion.8
  195.2 0.8 multiply_reduce_fusion.10
  196.0 37.2 %all-reduce = (f32[1]{0:T(128)}, f32[1]{0:T(128)}, f32[1]{0:T(128)}, f32[1]{0:T(128)}) all-reduce(f32[1]{0:T(128)} %bitcast.117, f32[1]{0:T(128)} %bitcast.101, f32[1]{0:T(128)} %bitcast.85, f32[1]{0:T(128)} %bitcast.69), channel_id=1, replica_groups=mesh['att'=8,'emb'=4] {'att','emb'}, use_global_device_ids=true, to_apply=%region_79.0 | all-reduce | flops 4 | bytes 32 | tf_op jit(solution)/shard_map/psum | solution.py:32
  238.7 1.4 bitcast_subtract_fusion.7
  240.3 1.5 pad_maximum_fusion.1
  241.8 0.6 pad_maximum_fusion.4
  242.4 5.1 %fusion.104 = (f32[1,3,512,256]{3,2,1,0:T(8,128)}, f32[1,3,512,256]{3,2,1,0:T(8,128)S(1)}, f32[1,3,512,256]{3,2,1,0:T(8,128)}, f32[1,3,512,256]{3,2,1,0:T(8,128)}) fusion(f32[4,3,512,256]{3,2,1,0:T(8,128)} %param.11), kind=kLoop, calls=%fused_computation.202 | loop fusion | bytes 12582912 | tf_op jit(solution)/shard_map/slice | solution.py:71
  247.6 1.9 copy.59
  249.7 0.9 copy-done
  250.6 0.5 copy.67
  251.4 1.9 copy.63
  253.5 0.9 copy-done.1
  254.4 1.9 copy.71
  256.5 41.5 %all-reduce.3 = (f32[3,3]{0,1:T(4,128)S(1)}, f32[3,3]{0,1:T(4,128)S(1)}, f32[3,3]{0,1:T(4,128)S(1)}, f32[3,3]{0,1:T(4,128)S(1)}) all-reduce(f32[3,3]{0,1:T(4,128)S(1)} %pad_maximum_fusion.9, f32[3,3]{0,1:T(4,128)S(1)} %pad_maximum_fusion.8, f32[3,3]{0,1:T(4,128)S(1)} %pad_maximum_fusion.7, ...), channel_id=1, replica_groups=mesh['att'=8,'emb'=4] {'emb','att'}, use_global_device_ids=true, to_apply=%region_33.0 | all-reduce | flops 36 | bytes 288 | tf_op jit(solution)/shard_map/psum | solution.py:24
  298.1 0.8 add_bitcast_fusion
  298.8 0.7 add_bitcast_fusion.1
  299.5 0.7 add_bitcast_fusion.2
  300.2 0.7 add_bitcast_fusion.3
  300.8 0.7 fusion.88
  301.6 1.9 multiply_reduce_fusion.3
  303.5 0.4 multiply_reduce_fusion.2
  304.0 0.8 fusion.90
  304.7 0.6 copy.57
  305.4 0.4 multiply_reduce_fusion.1
  305.8 0.4 multiply_reduce_fusion
  306.2 39.7 %all-reduce.2 = (f32[3]{0:T(128)S(1)}, f32[3]{0:T(128)S(1)}, f32[3]{0:T(128)S(1)}, f32[3]{0:T(128)S(1)}) all-reduce(f32[3]{0:T(128)S(1)} %multiply_reduce_fusion, f32[3]{0:T(128)S(1)} %multiply_reduce_fusion.1, f32[3]{0:T(128)S(1)} %multiply_reduce_fusion.2, ...), channel_id=1, replica_groups=mesh['att'=8,'emb'=4] {'emb','att'}, use_global_device_ids=true, to_apply=%region_39.0 | all-reduce | flops 12 | bytes 96 | tf_op jit(solution)/shard_map/psum | solution.py:32
  345.9 1.2 bitcast_divide_fusion.3
  347.1 2.3 fusion.46
  349.5 1.2 bitcast_divide_fusion.2
  350.7 0.3 fusion.44
  351.0 1.3 bitcast_divide_fusion.1
  352.3 0.3 fusion.42
  352.6 1.3 bitcast_divide_fusion
  354.0 0.3 fusion.40
  354.3 3.0 pad_maximum_fusion
  357.2 6.6 %copy.56 = f32[4,3,512,256]{3,2,1,0:T(8,128)} copy(f32[4,3,512,256]{2,3,1,0:T(8,128)} %pad_maximum_fusion) | data formatting | bytes 12582912
  (47 shorter events, 1.5 us)
Async XLA Ops:
  0.6 8.5 %copy-start.13 = (f32[4,3,256]{2,0,1:T(4,128)S(1)}, f32[4,3,256]{2,0,1:T(4,128)}, u32[]{:S(2)}) copy-start(f32[4,3,256]{2,0,1:T(4,128)} %param.18) | copy-start | bytes 36868
  0.6 8.5 %copy-start.11 = (f32[4,3,512]{2,0,1:T(4,128)S(1)}, f32[4,3,512]{2,0,1:T(4,128)}, u32[]{:S(2)}) copy-start(f32[4,3,512]{2,0,1:T(4,128)} %param.17) | copy-start | bytes 73732
  9.3 16.7 %copy-start.15 = (bf16[4,6144,512]{2,1,0:T(8,128)(2,1)S(1)}, bf16[4,6144,512]{2,1,0:T(8,128)(2,1)}, u32[]{:S(2)}) copy-start(bf16[4,6144,512]{2,1,0:T(8,128)(2,1)} %param.16) | copy-start | bytes 75497472
  127.8 59.6 %copy-start.12 = (f32[4,256]{1,0:T(4,128)S(1)}, f32[4,256]{1,0:T(4,128)}, u32[]{:S(2)}) copy-start(f32[4,256]{1,0:T(4,128)} %param.19) | copy-start | bytes 12292
  127.8 62.1 %copy-start.14 = (f32[4,512]{1,0:T(4,128)S(1)}, f32[4,512]{1,0:T(4,128)}, u32[]{:S(2)}) copy-start(f32[4,512]{1,0:T(4,128)} %param.20) | copy-start | bytes 24580
  139.0 99.8 %copy-start.3 = (f32[4,256,512]{2,1,0:T(8,128)S(1)}, f32[4,256,512]{2,1,0:T(8,128)}, u32[]{:S(2)}) copy-start(f32[4,256,512]{2,1,0:T(8,128)} %param.12) | copy-start | bytes 6291460
  238.7 1.4 copy-start.10
  249.5 1.1 copy-start
  253.2 1.1 copy-start.1
  298.1 5.4 %copy-start.6 = (f32[3,256,512]{2,1,0:T(8,128)S(1)}, f32[3,256,512]{2,1,0:T(8,128)}, u32[]{:S(2)}) copy-start(f32[3,256,512]{2,1,0:T(8,128)} %get-tuple-element.166) | copy-start | bytes 4718596
  301.6 3.8 %copy-start.8 = (f32[3,256,512]{2,1,0:T(8,128)S(1)}, f32[3,256,512]{2,1,0:T(8,128)}, u32[]{:S(2)}) copy-start(f32[3,256,512]{2,1,0:T(8,128)} %get-tuple-element.165) | copy-start | bytes 4718596
  303.5 2.3 copy-start.4
  347.1 3.5 copy-start.2
  347.1 3.5 copy-start.7
  350.7 1.6 copy-start.9
  352.3 1.7 copy-start.5
where the time goes:
time: 365 us; the launch traced here: 364 us
  blocking collectives  208 us (57%)
  matrix products  67.3 us (18%)
  other arithmetic  42.4 us (12%)
  local copies, waits for them, and re-layouts  23.5 us (6%)
  between operations  22.4 us (6%)
    psum x2, blocking collectives, factored_step(): scalar_sum = lax.psum(scalar_part, (m_axis, n_axis))  83.6 us
    psum x2, blocking collectives, factored_step(): u_sum = lax.psum(jnp.sum(update * update, axis=(1, 2)), (m_axis, n_axis))  76.9 us
    dot_general x4, matrix products, local_run(): jnp.einsum('td,ktn->kdn', x_in[layer_idx], dy_qkv[layer_idx], preferred_e...  44.2 us
    psum x1, blocking collectives, factored_step(): row_sum = lax.psum(row_part, n_axis)  37.4 us
    dot_general x4, matrix products, local_run(): jnp.einsum('ti,td->id', x_attn[layer_idx], dy_out[layer_idx], preferred_e...  23.1 us
    unnamed x39, local copies, waits for them, and re-layouts  15.7 us
    another operation x14, other arithmetic, local_run(): jnp.stack([layer_out[out_slot] for layer_out in per_layer])  11.7 us
    psum x1, blocking collectives, factored_step(): col_sum = lax.psum(col_part, m_axis)  10.4 us

commit v1 on v0

v1 whole, which is shorter than its diff:
```python
import functools

import jax
import jax.numpy as jnp
from jax import lax
from jax.experimental import pallas as pl
from jax.experimental.pallas import tpu as pltpu
from jax.sharding import PartitionSpec as P

EPS_SQUARE = 1e-30
EPS_SCALE = 1e-3
F32 = jnp.float32
BF16 = jnp.bfloat16
MESH = pl.DeviceIdType.MESH
TB = 1024
NA = 6
NB = 6
ATT = 8
EMB = 4


def rows_to_lanes(part):
    return jnp.sum(part.T, axis=0, keepdims=True)


def fold8(part):
    return jnp.sum(part.reshape(part.shape[0] // 8, 8, 128), axis=0)


def total(part):
    return jnp.sum(jnp.sum(part, axis=0, keepdims=True), axis=1, keepdims=True)


def step_kernel(
    n_layers, n_tokens, d_model,
    hyper, x_in, dy_qkv, x_attn, dy_out, w_qkv, w_out, r_qkv, c_qkv, r_out, c_out,
    u_qkv, u_out, wv_qkv, wv_out, scales, rn_qkv, cn_qkv, rn_out, cn_out,
    xb, dyb, xab, dob, rq, cq, ro, co, row_a, row_b,
    att_a, emb_a, att_b, emb_b, glob, old_a, old_ac, old_b, old_bc, payload,
    sem_a, sem_b, sem_w, sem_s, send_sem, recv_sem, send_g, recv_g,
):
    nb = n_tokens // TB
    me_att = lax.axis_index("att")
    me_emb = lax.axis_index("emb")

    def copies_a(g):
        l, i, s = g // nb, g % nb, g % NA
        t = pl.ds(pl.multiple_of(i * TB, TB), TB)
        return (
            pltpu.make_async_copy(x_in.at[l, t], xb.at[s], sem_a.at[s, 0]),
            pltpu.make_async_copy(dy_qkv.at[l, :, t], dyb.at[s], sem_a.at[s, 1]),
        )

    def copies_b(g):
        l, i, s = g // nb, g % nb, g % NB
        t = pl.ds(pl.multiple_of(i * TB, TB), TB)
        return (
            pltpu.make_async_copy(x_attn.at[l, t], xab.at[s], sem_b.at[s, 0]),
            pltpu.make_async_copy(dy_out.at[l, t], dob.at[s], sem_b.at[s, 1]),
        )

    def copies_w(l):
        return (
            pltpu.make_async_copy(w_qkv.at[l], wv_qkv.at[l], sem_w.at[l, 0]),
            pltpu.make_async_copy(w_out.at[l], wv_out.at[l], sem_w.at[l, 1]),
        )

    def start(copies):
        for copy in copies:
            copy.start()

    def wait(copies):
        for copy in copies:
            copy.wait()

    def send_att(buf, kind, l):
        for d in (4, 3, 5, 2, 6, 1, 7):
            pltpu.make_async_remote_copy(
                src_ref=buf.at[l, 0], dst_ref=buf.at[l, ATT - d],
                send_sem=send_sem.at[kind, l], recv_sem=recv_sem.at[kind, l],
                device_id={"att": lax.rem(me_att + d, ATT)}, device_id_type=MESH,
            ).start()

    def send_emb(buf, kind, l):
        for d in (2, 1, 3):
            pltpu.make_async_remote_copy(
                src_ref=buf.at[l, 0], dst_ref=buf.at[l, EMB - d],
                send_sem=send_sem.at[kind, l], recv_sem=recv_sem.at[kind, l],
                device_id={"emb": lax.rem(me_emb + d, EMB)}, device_id_type=MESH,
            ).start()

    def wait_group(buf, n, kind, l):
        others = buf.at[l, pl.ds(1, n - 1)]
        pltpu.make_async_copy(others, others, send_sem.at[kind, l]).wait()
        pltpu.make_async_copy(others, others, recv_sem.at[kind, l]).wait()

    for g in range(NA):
        start(copies_a(jnp.int32(g)))
        start(copies_b(jnp.int32(g)))
    small = [
        pltpu.make_async_copy(src, dst, sem_s.at[n])
        for n, (src, dst) in enumerate(((r_qkv, rq), (c_qkv, cq), (r_out, ro), (c_out, co)))
    ]
    start(small)

    barrier = pltpu.get_barrier_semaphore()
    for da in range(ATT):
        for de in range(EMB):
            if da or de:
                pl.semaphore_signal(
                    barrier, inc=1,
                    device_id={"att": lax.rem(me_att + da, ATT), "emb": lax.rem(me_emb + de, EMB)},
                    device_id_type=MESH,
                )
    payload[...] = jnp.zeros_like(payload)
    wait(small)
    for l in range(n_layers):
        for k in range(3):
            for j in range(4):
                old_a[l, k * 4 + j : k * 4 + j + 1, :] = rq[k, l : l + 1, j * 128 : (j + 1) * 128]
            for j in range(2):
                old_ac[l, k * 2 + j : k * 2 + j + 1, :] = cq[k, l : l + 1, j * 128 : (j + 1) * 128]
        for j in range(2):
            old_b[l, j : j + 1, :] = ro[l : l + 1, j * 128 : (j + 1) * 128]
        for j in range(4):
            old_bc[l, j : j + 1, :] = co[l : l + 1, j * 128 : (j + 1) * 128]
    pl.semaphore_wait(barrier, ATT * EMB - 1)

    beta = hyper[0]
    gain = 1.0 - beta

    def zero(l):
        u_qkv[l] = jnp.zeros_like(u_qkv[l])
        u_out[l] = jnp.zeros_like(u_out[l])

    def mul_a(l, s):
        grads = jnp.concatenate([dyb[s, k] for k in range(3)], axis=1)
        prod = lax.dot_general(xb[s], grads, (((0,), (0,)), ((), ())), preferred_element_type=F32)
        for k in range(3):
            u_qkv[l, k] = u_qkv[l, k] + prod[:, k * 256 : (k + 1) * 256]

    def mul_b(l, s):
        prod = lax.dot_general(xab[s], dob[s], (((0,), (0,)), ((), ())), preferred_element_type=F32)
        u_out[l] = u_out[l] + prod

    def refill_a(g):
        @pl.when(g + NA < n_layers * nb)
        def _():
            start(copies_a(g + NA))

    def refill_b(g):
        @pl.when(g + NB < n_layers * nb)
        def _():
            start(copies_b(g + NB))

    def stats_a(l):
        for k in range(3):
            cols = None
            for q in range(2):
                g = u_qkv[l, k, pl.ds(q * 256, 256)]
                sq = g * g
                row_a[k, pl.ds(q * 256, 256)] = sq[:, :128] + sq[:, 128:]
                part = jnp.sum(sq, axis=0, keepdims=True)
                cols = part if cols is None else cols + part
            for j in range(2):
                emb_a[l, 0, k * 2 + j : k * 2 + j + 1, :] = cols[:, j * 128 : (j + 1) * 128]
        for k in range(3):
            rows = rows_to_lanes(row_a[k])
            for j in range(4):
                att_a[l, 0, k * 4 + j : k * 4 + j + 1, :] = rows[:, j * 128 : (j + 1) * 128]
        send_att(att_a, 0, l)
        send_emb(emb_a, 1, l)

    def stats_b(l):
        parts = []
        for q in range(2):
            g = u_out[l, :, pl.ds(q * 256, 256)]
            sq = g * g
            parts.append(sq[:, :128] + sq[:, 128:])
            cols = jnp.sum(sq, axis=0, keepdims=True)
            for j in range(2):
                att_b[l, 0, q * 2 + j : q * 2 + j + 1, :] = cols[:, j * 128 : (j + 1) * 128]
            if q == 0:
                row_b[...] = parts[0]
            else:
                row_b[...] = row_b[...] + parts[1]
        rows = rows_to_lanes(row_b[...])
        for j in range(2):
            emb_b[l, 0, j : j + 1, :] = rows[:, j * 128 : (j + 1) * 128]
        send_att(att_b, 2, l)
        send_emb(emb_b, 3, l)

    def record(slot, value):
        lane = lax.broadcasted_iota(jnp.int32, (1, 128), 1)
        payload[...] = jnp.where(lane == slot, value, payload[...])

    def sum_w(l):
        wait(copies_w(l))
        for k in range(3):
            w = wv_qkv[l, k]
            record(32 + l * 4 + k, total(fold8(w[:, :128] * w[:, :128] + w[:, 128:] * w[:, 128:])))
        w = wv_out[l]
        part = sum(fold8(w[:, j * 128 : (j + 1) * 128] * w[:, j * 128 : (j + 1) * 128]) for j in range(4))
        record(32 + l * 4 + 3, total(part))

    def apply_a(l):
        wait_group(att_a, ATT, 0, l)
        wait_group(emb_a, EMB, 1, l)
        row_sum = att_a[l, 0]
        for d in range(1, ATT):
            row_sum = row_sum + att_a[l, d]
        col_sum = emb_a[l, 0]
        for d in range(1, EMB):
            col_sum = col_sum + emb_a[l, d]
        r_new = beta * old_a[l] + gain * (row_sum * (1.0 / d_model) + EPS_SQUARE)
        c_new = beta * old_ac[l] + gain * (col_sum * (1.0 / d_model) + EPS_SQUARE)
        rn_qkv[l] = r_new
        cn_qkv[l] = c_new
        b_all = lax.rsqrt(c_new)
        for k in range(3):
            r_k = r_new[k * 4 : (k + 1) * 4]
            mean = total(r_k) * (1.0 / 512)
            a_k = lax.rsqrt(r_k / mean)
            tsum = jnp.zeros((8, 128), F32)
            for j in range(4):
                a_col = jnp.broadcast_to(a_k[j : j + 1], (128, 128)).T
                for h in range(2):
                    rr, cc = pl.ds(j * 128, 128), pl.ds(h * 128, 128)
                    u = u_qkv[l, k, rr, cc] * a_col * b_all[k * 2 + h : k * 2 + h + 1]
                    u_qkv[l, k, rr, cc] = u
                    tsum = tsum + fold8(u * u)
            record(l * 4 + k, total(tsum))
            record(16 + l * 4 + k, mean)

    def apply_b(l):
        wait_group(att_b, ATT, 2, l)
        wait_group(emb_b, EMB, 3, l)
        col_sum = att_b[l, 0]
        for d in range(1, ATT):
            col_sum = col_sum + att_b[l, d]
        row_sum = emb_b[l, 0]
        for d in range(1, EMB):
            row_sum = row_sum + emb_b[l, d]
        r_new = beta * old_b[l] + gain * (row_sum * (1.0 / d_model) + EPS_SQUARE)
        c_new = beta * old_bc[l] + gain * (col_sum * (1.0 / d_model) + EPS_SQUARE)
        b_all = lax.rsqrt(c_new)
        mean = total(r_new) * (1.0 / 256)
        a_all = lax.rsqrt(r_new / mean)
        tsum = jnp.zeros((8, 128), F32)
        for j in range(2):
            a_col = jnp.broadcast_to(a_all[j : j + 1], (128, 128)).T
            for h in range(4):
                rr, cc = pl.ds(j * 128, 128), pl.ds(h * 128, 128)
                u = u_out[l, rr, cc] * a_col * b_all[h : h + 1]
                u_out[l, rr, cc] = u
                tsum = tsum + fold8(u * u)
        rn_out[l] = r_new
        cn_out[l] = c_new
        record(l * 4 + 3, total(tsum))
        record(16 + l * 4 + 3, mean)

    last = n_layers - 1

    def layer(l, carry):
        start(copies_w(l))
        zero(l)

        def block(i, carry):
            g = l * nb + i
            wait(copies_a(g))
            wait(copies_b(g))
            mul_a(l, g % NA)
            mul_b(l, g % NB)
            refill_a(g)
            refill_b(g)

            @pl.when((i == 3) & (l > 0))
            def _():
                sum_w(l - 1)
                apply_a(l - 1)
                apply_b(l - 1)

            return carry

        lax.fori_loop(0, nb, block, 0)
        stats_a(l)
        stats_b(l)
        return carry

    lax.fori_loop(0, last, layer, 0)
    start(copies_w(last))
    zero(last)

    def block_a(i, carry):
        g = last * nb + i
        wait(copies_a(g))
        mul_a(last, g % NA)

        @pl.when(i == 3)
        def _():
            sum_w(last - 1)
            apply_a(last - 1)
            apply_b(last - 1)

        return carry

    lax.fori_loop(0, nb, block_a, 0)
    stats_a(last)

    def block_b(i, carry):
        g = last * nb + i
        wait(copies_b(g))
        mul_b(last, g % NB)
        return carry

    lax.fori_loop(0, nb, block_b, 0)
    stats_b(last)
    sum_w(last)
    apply_a(last)
    apply_b(last)

    glob[0] = payload[...]
    for da in (4, 3, 5, 2, 6, 1, 7, 0):
        for de in (2, 3, 1, 0):
            if da or de:
                pltpu.make_async_remote_copy(
                    src_ref=glob.at[0], dst_ref=glob.at[((ATT - da) % ATT) * EMB + (EMB - de) % EMB],
                    send_sem=send_g, recv_sem=recv_g,
                    device_id={"att": lax.rem(me_att + da, ATT), "emb": lax.rem(me_emb + de, EMB)},
                    device_id_type=MESH,
                ).start()
    others = glob.at[pl.ds(1, ATT * EMB - 1)]
    pltpu.make_async_copy(others, others, send_g).wait()
    pltpu.make_async_copy(others, others, recv_g).wait()
    n_dev = ATT * EMB
    mean_sum = jnp.zeros((1, 128), F32)
    w_sum = jnp.zeros((1, 128), F32)
    u_sum = jnp.zeros((1, 128), F32)
    for d in range(n_dev):
        row = glob[d]
        local_mean = pltpu.roll(row, 128 - 16, 1)
        mean_sum = mean_sum + local_mean
        w_sum = w_sum + pltpu.roll(row, 128 - 32, 1)
    mean_all = mean_sum * (1.0 / n_dev)
    for d in range(n_dev):
        row = glob[d]
        u_sum = u_sum + row * (mean_all / pltpu.roll(row, 128 - 16, 1))
    n_elems = float(d_model) * d_model
    rms_u = jnp.sqrt(u_sum * (1.0 / n_elems))
    rms_w = jnp.sqrt(w_sum * (1.0 / n_elems))
    step = hyper[1] * jnp.maximum(EPS_SCALE, rms_w) / jnp.maximum(1.0, rms_u / hyper[2])
    scales[...] = step * jnp.sqrt(mean_all / pltpu.roll(payload[...], 128 - 16, 1))


def write_kernel(
    n_layers, u_qkv, u_out, wv_qkv, wv_out, scales, rn_qkv, cn_qkv, rn_out, cn_out,
    wn_qkv, wn_out, r_qkv, c_qkv, r_out, c_out,
    st_a, st_b, st_rq, st_cq, st_r, st_c, sem_w, sem_s,
):
    for l in range(n_layers):
        for k in range(3):
            for j in range(4):
                st_rq[k, l : l + 1, j * 128 : (j + 1) * 128] = rn_qkv[l, k * 4 + j : k * 4 + j + 1]
            for j in range(2):
                st_cq[k, l : l + 1, j * 128 : (j + 1) * 128] = cn_qkv[l, k * 2 + j : k * 2 + j + 1]
        for j in range(2):
            st_r[l : l + 1, j * 128 : (j + 1) * 128] = rn_out[l, j : j + 1]
        for j in range(4):
            st_c[l : l + 1, j * 128 : (j + 1) * 128] = cn_out[l, j : j + 1]
    small = [
        pltpu.make_async_copy(src, dst, sem_s.at[n])
        for n, (src, dst) in enumerate(((st_rq, r_qkv), (st_cq, c_qkv), (st_r, r_out), (st_c, c_out)))
    ]
    for copy in small:
        copy.start()
    copies = []
    for l in range(n_layers):
        for k in range(4):
            m = l * 4 + k
            s = scales[0:1, m : m + 1]
            if k < 3:
                st_a[l, k] = wv_qkv[l, k] - s * u_qkv[l, k]
                copy = pltpu.make_async_copy(st_a.at[l, k], wn_qkv.at[l, k], sem_w.at[m])
            else:
                st_b[l] = wv_out[l] - s * u_out[l]
                copy = pltpu.make_async_copy(st_b.at[l], wn_out.at[l], sem_w.at[m])
            copy.start()
            copies.append(copy)
    for copy in copies + small:
        copy.wait()


def solution(mesh):
    att, emb = mesh.shape["att"], mesh.shape["emb"]
    qkv = P(None, None, "emb", "att")
    out = P(None, "att", "emb")
    row = P(None, None, "emb")
    col = P(None, None, "att")

    def local_run(w_qkv, w_out, x_in, dy_qkv, x_attn, dy_out, r_qkv, c_qkv, r_out, c_out, hyper_params):
        n_layers, n_tokens = x_in.shape[:2]
        d_model = x_in.shape[2] * emb
        hbm = pl.BlockSpec(memory_space=pltpu.HBM)
        vmem = pl.BlockSpec(memory_space=pltpu.VMEM)
        smem = pl.BlockSpec(memory_space=pltpu.SMEM)
        like = lambda x: jax.ShapeDtypeStruct(x.shape, x.dtype)
        kept = lambda x: pltpu.VMEM(x.shape, x.dtype)
        stat = lambda n: pltpu.VMEM((n_layers, n, 128), F32)
        r_qkv, c_qkv = jnp.swapaxes(r_qkv, 0, 1), jnp.swapaxes(c_qkv, 0, 1)
        mids = pl.pallas_call(
            functools.partial(step_kernel, n_layers, n_tokens, d_model),
            out_shape=(
                kept(w_qkv), kept(w_out), kept(w_qkv), kept(w_out), pltpu.VMEM((1, 128), F32),
                stat(12), stat(6), stat(2), stat(4),
            ),
            in_specs=[smem] + [hbm] * 10,
            out_specs=[vmem] * 9,
            scratch_shapes=[
                pltpu.VMEM((NA, TB, 512), BF16), pltpu.VMEM((NA, 3, TB, 256), BF16),
                pltpu.VMEM((NB, TB, 256), BF16), pltpu.VMEM((NB, TB, 512), BF16),
                pltpu.VMEM(r_qkv.shape, F32), pltpu.VMEM(c_qkv.shape, F32),
                pltpu.VMEM(r_out.shape, F32), pltpu.VMEM(c_out.shape, F32),
                pltpu.VMEM((3, 512, 128), F32), pltpu.VMEM((256, 128), F32),
                pltpu.VMEM((n_layers, ATT, 12, 128), F32), pltpu.VMEM((n_layers, EMB, 6, 128), F32),
                pltpu.VMEM((n_layers, ATT, 4, 128), F32), pltpu.VMEM((n_layers, EMB, 2, 128), F32),
                pltpu.VMEM((ATT * EMB, 1, 128), F32),
                pltpu.VMEM((n_layers, 12, 128), F32), pltpu.VMEM((n_layers, 6, 128), F32),
                pltpu.VMEM((n_layers, 2, 128), F32), pltpu.VMEM((n_layers, 4, 128), F32),
                pltpu.VMEM((1, 128), F32),
                pltpu.SemaphoreType.DMA((NA, 2)), pltpu.SemaphoreType.DMA((NB, 2)),
                pltpu.SemaphoreType.DMA((n_layers, 2)), pltpu.SemaphoreType.DMA((4,)),
                pltpu.SemaphoreType.DMA((4, n_layers)), pltpu.SemaphoreType.DMA((4, n_layers)),
                pltpu.SemaphoreType.DMA, pltpu.SemaphoreType.DMA,
            ],
            compiler_params=pltpu.CompilerParams(
                collective_id=0, has_side_effects=True, vmem_limit_bytes=45 * 2**20
            ),
            name="adafactor_step",
        )(hyper_params, x_in, dy_qkv, x_attn, dy_out, w_qkv, w_out, r_qkv, c_qkv, r_out, c_out)
        wn_qkv, wn_out, rn_qkv, cn_qkv, rn_out, cn_out = pl.pallas_call(
            functools.partial(write_kernel, n_layers),
            out_shape=(like(w_qkv), like(w_out), like(r_qkv), like(c_qkv), like(r_out), like(c_out)),
            in_specs=[vmem] * 9,
            out_specs=[hbm] * 6,
            scratch_shapes=[
                pltpu.VMEM(w_qkv.shape, F32), pltpu.VMEM(w_out.shape, F32),
                pltpu.VMEM(r_qkv.shape, F32), pltpu.VMEM(c_qkv.shape, F32),
                pltpu.VMEM(r_out.shape, F32), pltpu.VMEM(c_out.shape, F32),
                pltpu.SemaphoreType.DMA((4 * n_layers,)), pltpu.SemaphoreType.DMA((4,)),
            ],
            compiler_params=pltpu.CompilerParams(vmem_limit_bytes=16 * 2**20),
            name="adafactor_write",
        )(*mids)
        return wn_qkv, wn_out, jnp.swapaxes(rn_qkv, 0, 1), jnp.swapaxes(cn_qkv, 0, 1), rn_out, cn_out

    return jax.shard_map(
        local_run,
        mesh=mesh,
        in_specs=(qkv, out, row, P(None, None, None, "att"), col, row, row, col, P(None, "att"), P(None, "emb"), P()),
        out_specs=(qkv, out, row, col, P(None, "att"), P(None, "emb")),
        check_vma=False,
    )
```

time: 365 us -> 64.9 us (0.18)
  blocking collectives: 208 us -> 0 us
  matrix products: 67.3 us -> 0 us
  Pallas kernels: 0 us -> 64 us
  other arithmetic: 42.4 us -> 0 us
  local copies, waits for them, and re-layouts: 23.5 us -> 0 us
  between operations: 22.4 us -> 0.64 us
    psum x6 -> x0, blocking collectives: 208 us -> none  [the longest x2 83.6 us: factored_step(): scalar_sum = lax.psum(scalar_part, (m_axis, n_axis))]
    dot_general x8 -> x0, matrix products: 67.3 us -> none  [the longest x4 44.2 us: local_run(): jnp.einsum('td,ktn->kdn', x_in[layer_idx], dy_qkv[layer_idx], preferred_e...]
    pallas_call x0 -> x2, Pallas kernels: none -> 64 us  [the longest x1 60.4 us: local_run(): pl.pallas_call(functools.partial(step_kernel, n_layers, n_tokens, d_model...]
    another operation x22 -> x0, other arithmetic: 18.1 us -> none  [the longest x14 11.7 us: local_run(): jnp.stack([layer_out[out_slot] for layer_out in per_layer])]
    unnamed x39 -> x0, local copies, waits for them, and re-layouts: 15.7 us -> none
    reduce_sum x15 -> x0, other arithmetic: 13.6 us -> none  [the longest x8 8.66 us: factored_step(): u_sum = lax.psum(jnp.sum(update * update, axis=(1, 2)), (m_axis, n_axis))]
    slice x5 -> x0, local copies, waits for them, and re-layouts: 7.82 us -> none  [the longest x1 5.14 us: local_run(): w_qkv[layer_idx]]
    div x8 -> x0, other arithmetic: 7.73 us -> none  [the longest x4 5 us: factored_step(): rel_step * jnp.maximum(EPS_SCALE, rms_w)]
where the time goes in v1:
time: 64.9 us; the launch traced here: 64.7 us
  Pallas kernels  64 us (99%)
    pallas_call x1, Pallas kernels, local_run(): pl.pallas_call(functools.partial(step_kernel, n_layers, n_tokens, d_model...  60.4 us
    pallas_call x1, Pallas kernels, local_run(): pl.pallas_call(functools.partial(write_kernel, n_layers), out_shape=(like...  3.62 us

profile of v1, /device:TPU:0, one launch (start us, length us, event | category | flops | bytes accessed | tf_op | source)
XLA Modules:
  0.0 64.7 jit_solution(3545571055984178262)
XLA Ops:
  0.6 60.4 %adafactor_step.1 = (f32[4,3,512,256]{3,2,1,0:T(8,128)S(1)}, f32[4,256,512]{2,1,0:T(8,128)S(1)}, f32[4,3,512,256]{3,2,1,0:T(8,128)S(1)}, f32[4,256,512]{2,1,0:T(...) custom-call(f32[3]{0:T(128)} %hyper.1, ...), custom_call_target="tpu_custom_call" | custom-call | tf_op jit(solution)/shard_map/adafactor_step/pallas_call | solution.py:410
  61.0 3.6 %adafactor_write.1 = (f32[4,3,512,256]{3,2,1,0:T(8,128)}, f32[4,256,512]{2,1,0:T(8,128)}, f32[3,4,512]{2,1,0:T(4,128)}, f32[3,4,256]{2,1,0:T(4,128)}, f32[4,256]{1,0:T(4,128)}, /*index=5*/f32[4,512]{1,0:T(4,128)}) custom-call(f32[4,3,512,256]{3,2,1,0:T(8,128)S(1)} %get-tuple-element.21.u_qkv, f32[4,256,512]{2,1,0:T(8,128)S(1)} %get-tuple-element.22.u_out, ...), custom_call_target="tpu_custom_call" | custom-call | tf_op jit(solution)/shard_map/adafactor_write/pallas_call | solution.py:440

commit v2 on v1

--- a/solution.py
+++ b/solution.py
@@ -12,9 +12,9 @@
 F32 = jnp.float32
 BF16 = jnp.bfloat16
 MESH = pl.DeviceIdType.MESH
-TB = 1024
-NA = 6
-NB = 6
+TB = 2048
+NA = 3
+NB = 3
 ATT = 8
 EMB = 4
 
@@ -94,14 +94,14 @@
         pltpu.make_async_copy(others, others, send_sem.at[kind, l]).wait()
         pltpu.make_async_copy(others, others, recv_sem.at[kind, l]).wait()
 
-    for g in range(NA):
-        start(copies_a(jnp.int32(g)))
-        start(copies_b(jnp.int32(g)))
     small = [
         pltpu.make_async_copy(src, dst, sem_s.at[n])
         for n, (src, dst) in enumerate(((r_qkv, rq), (c_qkv, cq), (r_out, ro), (c_out, co)))
     ]
     start(small)
+    for g in range(NA):
+        start(copies_a(jnp.int32(g)))
+        start(copies_b(jnp.int32(g)))
 
     barrier = pltpu.get_barrier_semaphore()
     for da in range(ATT):
@@ -113,21 +113,23 @@
                     device_id_type=MESH,
                 )
     payload[...] = jnp.zeros_like(payload)
-    wait(small)
-    for l in range(n_layers):
-        for k in range(3):
-            for j in range(4):
-                old_a[l, k * 4 + j : k * 4 + j + 1, :] = rq[k, l : l + 1, j * 128 : (j + 1) * 128]
-            for j in range(2):
-                old_ac[l, k * 2 + j : k * 2 + j + 1, :] = cq[k, l : l + 1, j * 128 : (j + 1) * 128]
-        for j in range(2):
-            old_b[l, j : j + 1, :] = ro[l : l + 1, j * 128 : (j + 1) * 128]
-        for j in range(4):
-            old_bc[l, j : j + 1, :] = co[l : l + 1, j * 128 : (j + 1) * 128]
-    pl.semaphore_wait(barrier, ATT * EMB - 1)
 
     beta = hyper[0]
     gain = 1.0 - beta
+
+    def prepare():
+        wait(small)
+        for l in range(n_layers):
+            for k in range(3):
+                for j in range(4):
+                    old_a[l, k * 4 + j : k * 4 + j + 1, :] = rq[k, l : l + 1, j * 128 : (j + 1) * 128]
+                for j in range(2):
+                    old_ac[l, k * 2 + j : k * 2 + j + 1, :] = cq[k, l : l + 1, j * 128 : (j + 1) * 128]
+            for j in range(2):
+                old_b[l, j : j + 1, :] = ro[l : l + 1, j * 128 : (j + 1) * 128]
+            for j in range(4):
+                old_bc[l, j : j + 1, :] = co[l : l + 1, j * 128 : (j + 1) * 128]
+        pl.semaphore_wait(barrier, ATT * EMB - 1)
 
     def zero(l):
         u_qkv[l] = jnp.zeros_like(u_qkv[l])
@@ -262,7 +264,6 @@
     last = n_layers - 1
 
     def layer(l, carry):
-        start(copies_w(l))
         zero(l)
 
         def block(i, carry):
@@ -273,38 +274,36 @@
             mul_b(l, g % NB)
             refill_a(g)
             refill_b(g)
-
-            @pl.when((i == 3) & (l > 0))
-            def _():
-                sum_w(l - 1)
-                apply_a(l - 1)
-                apply_b(l - 1)
-
             return carry
 
         lax.fori_loop(0, nb, block, 0)
+
+        @pl.when(l == 0)
+        def _():
+            prepare()
+
         stats_a(l)
         stats_b(l)
+
+        @pl.when(l > 0)
+        def _():
+            apply_a(l - 1)
+            apply_b(l - 1)
+
         return carry
 
     lax.fori_loop(0, last, layer, 0)
-    start(copies_w(last))
     zero(last)
 
     def block_a(i, carry):
         g = last * nb + i
         wait(copies_a(g))
         mul_a(last, g % NA)
-
-        @pl.when(i == 3)
-        def _():
-            sum_w(last - 1)
-            apply_a(last - 1)
-            apply_b(last - 1)
-
         return carry
 
     lax.fori_loop(0, nb, block_a, 0)
+    for l in range(n_layers):
+        start(copies_w(l))
     stats_a(last)
 
     def block_b(i, carry):
@@ -315,7 +314,10 @@
 
     lax.fori_loop(0, nb, block_b, 0)
     stats_b(last)
-    sum_w(last)
+    apply_a(last - 1)
+    apply_b(last - 1)
+    for l in range(n_layers):
+        sum_w(l)
     apply_a(last)
     apply_b(last)
 

time: 64.9 us -> 54 us (0.83)
  Pallas kernels: 64 us -> 53.2 us
    pallas_call x1, Pallas kernels: 60.4 us -> 49.5 us  [local_run(): pl.pallas_call(functools.partial(step_kernel, n_layers, n_tokens, d_model...]
where the time goes in v2:
time: 54 us; the launch traced here: 53.8 us
  Pallas kernels  53.2 us (99%)
  between operations  0.64 us (1%)
    pallas_call x1, Pallas kernels, local_run(): pl.pallas_call(functools.partial(step_kernel, n_layers, n_tokens, d_model...  49.5 us
    pallas_call x1, Pallas kernels, local_run(): pl.pallas_call(functools.partial(write_kernel, n_layers), out_shape=(like...  3.62 us

profile of v2, /device:TPU:0, one launch (start us, length us, event | category | flops | bytes accessed | tf_op | source)
XLA Modules:
  0.0 53.8 jit_solution(3341731364381535673)
XLA Ops:
  0.6 49.5 %adafactor_step.1 = (f32[4,3,512,256]{3,2,1,0:T(8,128)S(1)}, f32[4,256,512]{2,1,0:T(8,128)S(1)}, f32[4,3,512,256]{3,2,1,0:T(8,128)S(1)}, f32[4,256,512]{2,1,0:T(...) custom-call(f32[3]{0:T(128)} %hyper.1, ...), custom_call_target="tpu_custom_call" | custom-call | tf_op jit(solution)/shard_map/adafactor_step/pallas_call | solution.py:412
  50.2 3.6 %adafactor_write.1 = (f32[4,3,512,256]{3,2,1,0:T(8,128)}, f32[4,256,512]{2,1,0:T(8,128)}, f32[3,4,512]{2,1,0:T(4,128)}, f32[3,4,256]{2,1,0:T(4,128)}, f32[4,256]{1,0:T(4,128)}, /*index=5*/f32[4,512]{1,0:T(4,128)}) custom-call(f32[4,3,512,256]{3,2,1,0:T(8,128)S(1)} %get-tuple-element.21.u_qkv, f32[4,256,512]{2,1,0:T(8,128)S(1)} %get-tuple-element.22.u_out, ...), custom_call_target="tpu_custom_call" | custom-call | tf_op jit(solution)/shard_map/adafactor_write/pallas_call | solution.py:442

commit v3 on v2

--- a/solution.py
+++ b/solution.py
@@ -13,6 +13,7 @@
 BF16 = jnp.bfloat16
 MESH = pl.DeviceIdType.MESH
 TB = 2048
+SUB = 2048
 NA = 3
 NB = 3
 ATT = 8
@@ -43,21 +44,25 @@
     me_att = lax.axis_index("att")
     me_emb = lax.axis_index("emb")
 
-    def copies_a(g):
+    def copies_a(g, subs=range(TB // SUB)):
         l, i, s = g // nb, g % nb, g % NA
-        t = pl.ds(pl.multiple_of(i * TB, TB), TB)
-        return (
-            pltpu.make_async_copy(x_in.at[l, t], xb.at[s], sem_a.at[s, 0]),
-            pltpu.make_async_copy(dy_qkv.at[l, :, t], dyb.at[s], sem_a.at[s, 1]),
-        )
-
-    def copies_b(g):
+        copies = []
+        for n in subs:
+            src = pl.ds(pl.multiple_of(i * TB + n * SUB, SUB), SUB)
+            dst = pl.ds(n * SUB, SUB)
+            copies.append(pltpu.make_async_copy(x_in.at[l, src], xb.at[s, dst], sem_a.at[s, 2 * n]))
+            copies.append(pltpu.make_async_copy(dy_qkv.at[l, :, src], dyb.at[s, :, dst], sem_a.at[s, 2 * n + 1]))
+        return copies
+
+    def copies_b(g, subs=range(TB // SUB)):
         l, i, s = g // nb, g % nb, g % NB
-        t = pl.ds(pl.multiple_of(i * TB, TB), TB)
-        return (
-            pltpu.make_async_copy(x_attn.at[l, t], xab.at[s], sem_b.at[s, 0]),
-            pltpu.make_async_copy(dy_out.at[l, t], dob.at[s], sem_b.at[s, 1]),
-        )
+        copies = []
+        for n in subs:
+            src = pl.ds(pl.multiple_of(i * TB + n * SUB, SUB), SUB)
+            dst = pl.ds(n * SUB, SUB)
+            copies.append(pltpu.make_async_copy(x_attn.at[l, src], xab.at[s, dst], sem_b.at[s, 2 * n]))
+            copies.append(pltpu.make_async_copy(dy_out.at[l, src], dob.at[s, dst], sem_b.at[s, 2 * n + 1]))
+        return copies
 
     def copies_w(l):
         return (
@@ -99,7 +104,10 @@
         for n, (src, dst) in enumerate(((r_qkv, rq), (c_qkv, cq), (r_out, ro), (c_out, co)))
     ]
     start(small)
-    for g in range(NA):
+    for n in range(TB // SUB):
+        start(copies_a(jnp.int32(0), (n,)))
+        start(copies_b(jnp.int32(0), (n,)))
+    for g in range(1, NA):
         start(copies_a(jnp.int32(g)))
         start(copies_b(jnp.int32(g)))
 
@@ -131,19 +139,15 @@
                 old_bc[l, j : j + 1, :] = co[l : l + 1, j * 128 : (j + 1) * 128]
         pl.semaphore_wait(barrier, ATT * EMB - 1)
 
-    def zero(l):
-        u_qkv[l] = jnp.zeros_like(u_qkv[l])
-        u_out[l] = jnp.zeros_like(u_out[l])
-
-    def mul_a(l, s):
-        grads = jnp.concatenate([dyb[s, k] for k in range(3)], axis=1)
-        prod = lax.dot_general(xb[s], grads, (((0,), (0,)), ((), ())), preferred_element_type=F32)
-        for k in range(3):
-            u_qkv[l, k] = u_qkv[l, k] + prod[:, k * 256 : (k + 1) * 256]
-
-    def mul_b(l, s):
-        prod = lax.dot_general(xab[s], dob[s], (((0,), (0,)), ((), ())), preferred_element_type=F32)
-        u_out[l] = u_out[l] + prod
+    def mul_a(l, s, keep, part=slice(None)):
+        grads = jnp.concatenate([dyb[s, k, part] for k in range(3)], axis=1)
+        prod = lax.dot_general(xb[s, part], grads, (((0,), (0,)), ((), ())), preferred_element_type=F32)
+        for k in range(3):
+            u_qkv[l, k] = jnp.where(keep, u_qkv[l, k], 0.0) + prod[:, k * 256 : (k + 1) * 256]
+
+    def mul_b(l, s, keep, part=slice(None)):
+        prod = lax.dot_general(xab[s, part], dob[s, part], (((0,), (0,)), ((), ())), preferred_element_type=F32)
+        u_out[l] = jnp.where(keep, u_out[l], 0.0) + prod
 
     def refill_a(g):
         @pl.when(g + NA < n_layers * nb)
@@ -206,8 +210,6 @@
         record(32 + l * 4 + 3, total(part))
 
     def apply_a(l):
-        wait_group(att_a, ATT, 0, l)
-        wait_group(emb_a, EMB, 1, l)
         row_sum = att_a[l, 0]
         for d in range(1, ATT):
             row_sum = row_sum + att_a[l, d]
@@ -231,12 +233,10 @@
                     u = u_qkv[l, k, rr, cc] * a_col * b_all[k * 2 + h : k * 2 + h + 1]
                     u_qkv[l, k, rr, cc] = u
                     tsum = tsum + fold8(u * u)
-            record(l * 4 + k, total(tsum))
+            record(l * 4 + k, total(tsum) / mean)
             record(16 + l * 4 + k, mean)
 
     def apply_b(l):
-        wait_group(att_b, ATT, 2, l)
-        wait_group(emb_b, EMB, 3, l)
         col_sum = att_b[l, 0]
         for d in range(1, ATT):
             col_sum = col_sum + att_b[l, d]
@@ -258,25 +258,47 @@
                 tsum = tsum + fold8(u * u)
         rn_out[l] = r_new
         cn_out[l] = c_new
-        record(l * 4 + 3, total(tsum))
+        record(l * 4 + 3, total(tsum) / mean)
         record(16 + l * 4 + 3, mean)
 
     last = n_layers - 1
 
+    def arrive_a(l):
+        wait_group(att_a, ATT, 0, l)
+        wait_group(emb_a, EMB, 1, l)
+
+    def arrive_b(l):
+        wait_group(att_b, ATT, 2, l)
+        wait_group(emb_b, EMB, 3, l)
+
+    def piece(n, carry):
+        part = pl.ds(pl.multiple_of(n * SUB, SUB), SUB)
+        for m in range(TB // SUB):
+            @pl.when(n == m)
+            def _():
+                wait(copies_a(jnp.int32(0), (m,)))
+                wait(copies_b(jnp.int32(0), (m,)))
+
+        mul_a(0, 0, n > 0, part)
+        mul_b(0, 0, n > 0, part)
+        return carry
+
+    lax.fori_loop(0, TB // SUB, piece, 0)
+    refill_a(jnp.int32(0))
+    refill_b(jnp.int32(0))
+
     def layer(l, carry):
-        zero(l)
-
         def block(i, carry):
             g = l * nb + i
             wait(copies_a(g))
             wait(copies_b(g))
-            mul_a(l, g % NA)
-            mul_b(l, g % NB)
+            mul_a(l, g % NA, i > 0)
+            mul_b(l, g % NB, i > 0)
             refill_a(g)
             refill_b(g)
             return carry
 
-        lax.fori_loop(0, nb, block, 0)
+        lax.fori_loop(jnp.where(l == 0, 1, 0), nb, block, 0)
 
         @pl.when(l == 0)
         def _():
@@ -284,21 +306,14 @@
 
         stats_a(l)
         stats_b(l)
-
-        @pl.when(l > 0)
-        def _():
-            apply_a(l - 1)
-            apply_b(l - 1)
-
         return carry
 
     lax.fori_loop(0, last, layer, 0)
-    zero(last)
 
     def block_a(i, carry):
         g = last * nb + i
         wait(copies_a(g))
-        mul_a(last, g % NA)
+        mul_a(last, g % NA, i > 0)
         return carry
 
     lax.fori_loop(0, nb, block_a, 0)
@@ -309,16 +324,29 @@
     def block_b(i, carry):
         g = last * nb + i
         wait(copies_b(g))
-        mul_b(last, g % NB)
+        mul_b(last, g % NB, i > 0)
         return carry
 
     lax.fori_loop(0, nb, block_b, 0)
     stats_b(last)
-    apply_a(last - 1)
-    apply_b(last - 1)
-    for l in range(n_layers):
+
+    def earlier(l, carry):
+        arrive_a(l)
+        arrive_b(l)
+        apply_a(l)
+        apply_b(l)
+        return carry
+
+    lax.fori_loop(0, last, earlier, 0)
+
+    def weights(l, carry):
         sum_w(l)
+        return carry
+
+    lax.fori_loop(0, n_layers, weights, 0)
+    arrive_a(last)
     apply_a(last)
+    arrive_b(last)
     apply_b(last)
 
     glob[0] = payload[...]
@@ -335,18 +363,12 @@
     pltpu.make_async_copy(others, others, send_g).wait()
     pltpu.make_async_copy(others, others, recv_g).wait()
     n_dev = ATT * EMB
-    mean_sum = jnp.zeros((1, 128), F32)
-    w_sum = jnp.zeros((1, 128), F32)
-    u_sum = jnp.zeros((1, 128), F32)
-    for d in range(n_dev):
-        row = glob[d]
-        local_mean = pltpu.roll(row, 128 - 16, 1)
-        mean_sum = mean_sum + local_mean
-        w_sum = w_sum + pltpu.roll(row, 128 - 32, 1)
-    mean_all = mean_sum * (1.0 / n_dev)
-    for d in range(n_dev):
-        row = glob[d]
-        u_sum = u_sum + row * (mean_all / pltpu.roll(row, 128 - 16, 1))
+    sums = glob[0]
+    for d in range(1, n_dev):
+        sums = sums + glob[d]
+    mean_all = pltpu.roll(sums, 128 - 16, 1) * (1.0 / n_dev)
+    w_sum = pltpu.roll(sums, 128 - 32, 1)
+    u_sum = sums * mean_all
     n_elems = float(d_model) * d_model
     rms_u = jnp.sqrt(u_sum * (1.0 / n_elems))
     rms_w = jnp.sqrt(w_sum * (1.0 / n_elems))
@@ -359,6 +381,22 @@
     wn_qkv, wn_out, r_qkv, c_qkv, r_out, c_out,
     st_a, st_b, st_rq, st_cq, st_r, st_c, sem_w, sem_s,
 ):
+    copies = []
+    for l in range(n_layers):
+        for k in range(4):
+            m = l * 4 + k
+            s = scales[0:1, m : m + 1]
+            parts = 4 if m == 0 else 1
+            for n in range(parts):
+                if k < 3:
+                    rows = pl.ds(n * (512 // parts), 512 // parts)
+                    st_a[l, k, rows] = wv_qkv[l, k, rows] - s * u_qkv[l, k, rows]
+                    copy = pltpu.make_async_copy(st_a.at[l, k, rows], wn_qkv.at[l, k, rows], sem_w.at[m if n == 0 else 15 + n])
+                else:
+                    st_b[l] = wv_out[l] - s * u_out[l]
+                    copy = pltpu.make_async_copy(st_b.at[l], wn_out.at[l], sem_w.at[m])
+                copy.start()
+                copies.append(copy)
     for l in range(n_layers):
         for k in range(3):
             for j in range(4):
@@ -375,19 +413,6 @@
     ]
     for copy in small:
         copy.start()
-    copies = []
-    for l in range(n_layers):
-        for k in range(4):
-            m = l * 4 + k
-            s = scales[0:1, m : m + 1]
-            if k < 3:
-                st_a[l, k] = wv_qkv[l, k] - s * u_qkv[l, k]
-                copy = pltpu.make_async_copy(st_a.at[l, k], wn_qkv.at[l, k], sem_w.at[m])
-            else:
-                st_b[l] = wv_out[l] - s * u_out[l]
-                copy = pltpu.make_async_copy(st_b.at[l], wn_out.at[l], sem_w.at[m])
-            copy.start()
-            copies.append(copy)
     for copy in copies + small:
         copy.wait()
 
@@ -429,7 +454,7 @@
                 pltpu.VMEM((n_layers, 12, 128), F32), pltpu.VMEM((n_layers, 6, 128), F32),
                 pltpu.VMEM((n_layers, 2, 128), F32), pltpu.VMEM((n_layers, 4, 128), F32),
                 pltpu.VMEM((1, 128), F32),
-                pltpu.SemaphoreType.DMA((NA, 2)), pltpu.SemaphoreType.DMA((NB, 2)),
+                pltpu.SemaphoreType.DMA((NA, 2 * TB // SUB)), pltpu.SemaphoreType.DMA((NB, 2 * TB // SUB)),
                 pltpu.SemaphoreType.DMA((n_layers, 2)), pltpu.SemaphoreType.DMA((4,)),
                 pltpu.SemaphoreType.DMA((4, n_layers)), pltpu.SemaphoreType.DMA((4, n_layers)),
                 pltpu.SemaphoreType.DMA, pltpu.SemaphoreType.DMA,
@@ -448,7 +473,7 @@
                 pltpu.VMEM(w_qkv.shape, F32), pltpu.VMEM(w_out.shape, F32),
                 pltpu.VMEM(r_qkv.shape, F32), pltpu.VMEM(c_qkv.shape, F32),
                 pltpu.VMEM(r_out.shape, F32), pltpu.VMEM(c_out.shape, F32),
-                pltpu.SemaphoreType.DMA((4 * n_layers,)), pltpu.SemaphoreType.DMA((4,)),
+                pltpu.SemaphoreType.DMA((4 * n_layers + 3,)), pltpu.SemaphoreType.DMA((4,)),
             ],
             compiler_params=pltpu.CompilerParams(vmem_limit_bytes=16 * 2**20),
             name="adafactor_write",

time: 54 us -> 52.8 us (0.978)
  Pallas kernels: 53.2 us -> 52 us
    pallas_call x1, Pallas kernels: 49.5 us -> 48.4 us  [local_run(): pl.pallas_call(functools.partial(step_kernel, n_layers, n_tokens, d_model...]
where the time goes in v3:
time: 52.8 us; the launch traced here: 52.6 us
  Pallas kernels  52 us (98%)
  between operations  0.64 us (1%)
    pallas_call x1, Pallas kernels, local_run(): pl.pallas_call(functools.partial(step_kernel, n_layers, n_tokens, d_model...  48.4 us
    pallas_call x1, Pallas kernels, local_run(): pl.pallas_call(functools.partial(write_kernel, n_layers), out_shape=(like...  3.59 us

profile of v3, /device:TPU:0, one launch (start us, length us, event | category | flops | bytes accessed | tf_op | source)
XLA Modules:
  0.0 52.6 jit_solution(3927183318324291093)
XLA Ops:
  0.6 48.4 %adafactor_step.1 = (f32[4,3,512,256]{3,2,1,0:T(8,128)S(1)}, f32[4,256,512]{2,1,0:T(8,128)S(1)}, f32[4,3,512,256]{3,2,1,0:T(8,128)S(1)}, f32[4,256,512]{2,1,0:T(...) custom-call(f32[3]{0:T(128)} %hyper.1, ...), custom_call_target="tpu_custom_call" | custom-call | tf_op jit(solution)/shard_map/adafactor_step/pallas_call | solution.py:437
  49.0 3.6 %adafactor_write.1 = (f32[4,3,512,256]{3,2,1,0:T(8,128)}, f32[4,256,512]{2,1,0:T(8,128)}, f32[3,4,512]{2,1,0:T(4,128)}, f32[3,4,256]{2,1,0:T(4,128)}, f32[4,256]{1,0:T(4,128)}, /*index=5*/f32[4,512]{1,0:T(4,128)}) custom-call(f32[4,3,512,256]{3,2,1,0:T(8,128)S(1)} %get-tuple-element.21.u_qkv, f32[4,256,512]{2,1,0:T(8,128)S(1)} %get-tuple-element.22.u_out, ...), custom_call_target="tpu_custom_call" | custom-call | tf_op jit(solution)/shard_map/adafactor_write/pallas_call | solution.py:467

commit v4 on v3

--- a/solution.py
+++ b/solution.py
@@ -36,7 +36,7 @@
     n_layers, n_tokens, d_model,
     hyper, x_in, dy_qkv, x_attn, dy_out, w_qkv, w_out, r_qkv, c_qkv, r_out, c_out,
     u_qkv, u_out, wv_qkv, wv_out, scales, rn_qkv, cn_qkv, rn_out, cn_out,
-    xb, dyb, xab, dob, rq, cq, ro, co, row_a, row_b,
+    xb, dyb, xab, dob, rq, cq, ro, co, row_a, row_b, a_cols, parts,
     att_a, emb_a, att_b, emb_b, glob, old_a, old_ac, old_b, old_bc, payload,
     sem_a, sem_b, sem_w, sem_s, send_sem, recv_sem, send_g, recv_g,
 ):
@@ -198,16 +198,15 @@
 
     def record(slot, value):
         lane = lax.broadcasted_iota(jnp.int32, (1, 128), 1)
-        payload[...] = jnp.where(lane == slot, value, payload[...])
+        payload[...] = jnp.where(lane == 8 * slot, value, payload[...])
 
     def sum_w(l):
         wait(copies_w(l))
         for k in range(3):
             w = wv_qkv[l, k]
-            record(32 + l * 4 + k, total(fold8(w[:, :128] * w[:, :128] + w[:, 128:] * w[:, 128:])))
+            parts[1, l * 4 + k] = fold8(w[:, :128] * w[:, :128] + w[:, 128:] * w[:, 128:])
         w = wv_out[l]
-        part = sum(fold8(w[:, j * 128 : (j + 1) * 128] * w[:, j * 128 : (j + 1) * 128]) for j in range(4))
-        record(32 + l * 4 + 3, total(part))
+        parts[1, l * 4 + 3] = sum(fold8(w[:, j * 128 : (j + 1) * 128] * w[:, j * 128 : (j + 1) * 128]) for j in range(4))
 
     def apply_a(l):
         row_sum = att_a[l, 0]
@@ -221,20 +220,22 @@
         rn_qkv[l] = r_new
         cn_qkv[l] = c_new
         b_all = lax.rsqrt(c_new)
-        for k in range(3):
-            r_k = r_new[k * 4 : (k + 1) * 4]
-            mean = total(r_k) * (1.0 / 512)
-            a_k = lax.rsqrt(r_k / mean)
+        means = [total(r_new[k * 4 : (k + 1) * 4]) * (1.0 / 512) for k in range(3)]
+        for k in range(3):
+            a_k = lax.rsqrt(r_new[k * 4 : (k + 1) * 4] / means[k])
+            for j in range(4):
+                a_cols[k * 4 + j] = jnp.broadcast_to(a_k[j : j + 1], (128, 128)).T
+        for k in range(3):
             tsum = jnp.zeros((8, 128), F32)
             for j in range(4):
-                a_col = jnp.broadcast_to(a_k[j : j + 1], (128, 128)).T
+                a_col = a_cols[k * 4 + j]
                 for h in range(2):
                     rr, cc = pl.ds(j * 128, 128), pl.ds(h * 128, 128)
                     u = u_qkv[l, k, rr, cc] * a_col * b_all[k * 2 + h : k * 2 + h + 1]
                     u_qkv[l, k, rr, cc] = u
                     tsum = tsum + fold8(u * u)
-            record(l * 4 + k, total(tsum) / mean)
-            record(16 + l * 4 + k, mean)
+            parts[0, l * 4 + k] = tsum
+            record(l * 4 + k, means[k])
 
     def apply_b(l):
         col_sum = att_b[l, 0]
@@ -258,10 +259,16 @@
                 tsum = tsum + fold8(u * u)
         rn_out[l] = r_new
         cn_out[l] = c_new
-        record(l * 4 + 3, total(tsum) / mean)
-        record(16 + l * 4 + 3, mean)
+        parts[0, l * 4 + 3] = tsum
+        record(l * 4 + 3, mean)
 
     last = n_layers - 1
+
+    def per_matrix(n):
+        sums = rows_to_lanes(parts[n].reshape(128, 128))
+        for shift in (4, 2, 1):
+            sums = sums + pltpu.roll(sums, 128 - shift, 1)
+        return sums
 
     def arrive_a(l):
         wait_group(att_a, ATT, 0, l)
@@ -346,10 +353,13 @@
     lax.fori_loop(0, n_layers, weights, 0)
     arrive_a(last)
     apply_a(last)
+    w_parts = per_matrix(1)
     arrive_b(last)
     apply_b(last)
 
-    glob[0] = payload[...]
+    phase = lax.broadcasted_iota(jnp.int32, (1, 128), 1) & 7
+    row = jnp.where(phase == 1, pltpu.roll(w_parts, 1, 1), pltpu.roll(payload[...], 2, 1))
+    glob[0] = jnp.where(phase == 0, per_matrix(0) / payload[...], row)
     for da in (4, 3, 5, 2, 6, 1, 7, 0):
         for de in (2, 3, 1, 0):
             if da or de:
@@ -366,14 +376,14 @@
     sums = glob[0]
     for d in range(1, n_dev):
         sums = sums + glob[d]
-    mean_all = pltpu.roll(sums, 128 - 16, 1) * (1.0 / n_dev)
-    w_sum = pltpu.roll(sums, 128 - 32, 1)
+    mean_all = pltpu.roll(sums, 128 - 2, 1) * (1.0 / n_dev)
+    w_sum = pltpu.roll(sums, 128 - 1, 1)
     u_sum = sums * mean_all
     n_elems = float(d_model) * d_model
     rms_u = jnp.sqrt(u_sum * (1.0 / n_elems))
     rms_w = jnp.sqrt(w_sum * (1.0 / n_elems))
     step = hyper[1] * jnp.maximum(EPS_SCALE, rms_w) / jnp.maximum(1.0, rms_u / hyper[2])
-    scales[...] = step * jnp.sqrt(mean_all / pltpu.roll(payload[...], 128 - 16, 1))
+    scales[...] = step * jnp.sqrt(mean_all / payload[...])
 
 
 def write_kernel(
@@ -385,7 +395,7 @@
     for l in range(n_layers):
         for k in range(4):
             m = l * 4 + k
-            s = scales[0:1, m : m + 1]
+            s = scales[0:1, 8 * m : 8 * m + 1]
             parts = 4 if m == 0 else 1
             for n in range(parts):
                 if k < 3:
@@ -448,6 +458,7 @@
                 pltpu.VMEM(r_qkv.shape, F32), pltpu.VMEM(c_qkv.shape, F32),
                 pltpu.VMEM(r_out.shape, F32), pltpu.VMEM(c_out.shape, F32),
                 pltpu.VMEM((3, 512, 128), F32), pltpu.VMEM((256, 128), F32),
+                pltpu.VMEM((12, 128, 128), F32), pltpu.VMEM((2, 4 * n_layers, 8, 128), F32),
                 pltpu.VMEM((n_layers, ATT, 12, 128), F32), pltpu.VMEM((n_layers, EMB, 6, 128), F32),
                 pltpu.VMEM((n_layers, ATT, 4, 128), F32), pltpu.VMEM((n_layers, EMB, 2, 128), F32),
                 pltpu.VMEM((ATT * EMB, 1, 128), F32),

time: 52.8 us -> 52.2 us (0.989)
  Pallas kernels: 52 us -> 51.4 us
    pallas_call x1, Pallas kernels: 48.4 us -> 47.8 us  [local_run(): pl.pallas_call(functools.partial(step_kernel, n_layers, n_tokens, d_model...]
where the time goes in v4:
time: 52.2 us; the launch traced here: 52 us
  Pallas kernels  51.4 us (98%)
  between operations  0.64 us (1%)
    pallas_call x1, Pallas kernels, local_run(): pl.pallas_call(functools.partial(step_kernel, n_layers, n_tokens, d_model...  47.8 us
    pallas_call x1, Pallas kernels, local_run(): pl.pallas_call(functools.partial(write_kernel, n_layers), out_shape=(like...  3.59 us

profile of v4, /device:TPU:0, one launch (start us, length us, event | category | flops | bytes accessed | tf_op | source)
XLA Modules:
  0.0 52.0 jit_solution(18000141825520725257)
XLA Ops:
  0.6 47.8 %adafactor_step.1 = (f32[4,3,512,256]{3,2,1,0:T(8,128)S(1)}, f32[4,256,512]{2,1,0:T(8,128)S(1)}, f32[4,3,512,256]{3,2,1,0:T(8,128)S(1)}, f32[4,256,512]{2,1,0:T(...) custom-call(f32[3]{0:T(128)} %hyper.1, ...), custom_call_target="tpu_custom_call" | custom-call | tf_op jit(solution)/shard_map/adafactor_step/pallas_call | solution.py:447
  48.4 3.6 %adafactor_write.1 = (f32[4,3,512,256]{3,2,1,0:T(8,128)}, f32[4,256,512]{2,1,0:T(8,128)}, f32[3,4,512]{2,1,0:T(4,128)}, f32[3,4,256]{2,1,0:T(4,128)}, f32[4,256]{1,0:T(4,128)}, /*index=5*/f32[4,512]{1,0:T(4,128)}) custom-call(f32[4,3,512,256]{3,2,1,0:T(8,128)S(1)} %get-tuple-element.21.u_qkv, f32[4,256,512]{2,1,0:T(8,128)S(1)} %get-tuple-element.22.u_out, ...), custom_call_target="tpu_custom_call" | custom-call | tf_op jit(solution)/shard_map/adafactor_write/pallas_call | solution.py:478

commit v5 on v4

--- a/solution.py
+++ b/solution.py
@@ -328,13 +328,10 @@
         start(copies_w(l))
     stats_a(last)
 
-    def block_b(i, carry):
-        g = last * nb + i
-        wait(copies_b(g))
-        mul_b(last, g % NB, i > 0)
-        return carry
-
-    lax.fori_loop(0, nb, block_b, 0)
+    for n in range(nb):
+        wait(copies_b(jnp.int32(last * nb + n)))
+    lhs, rhs = xab[...].reshape(n_tokens, 256), dob[...].reshape(n_tokens, 512)
+    u_out[last] = lax.dot_general(lhs, rhs, (((0,), (0,)), ((), ())), preferred_element_type=F32)
     stats_b(last)
 
     def earlier(l, carry):

time: 52.2 us -> 51.7 us (level)
  no operation moved by 1% of the time
where the time goes in v5:
time: 51.7 us; the launch traced here: 51.6 us
  Pallas kernels  50.9 us (98%)
  between operations  0.64 us (1%)
    pallas_call x1, Pallas kernels, local_run(): pl.pallas_call(functools.partial(step_kernel, n_layers, n_tokens, d_model...  47.3 us
    pallas_call x1, Pallas kernels, local_run(): pl.pallas_call(functools.partial(write_kernel, n_layers), out_shape=(like...  3.59 us

profile of v5, /device:TPU:0, one launch (start us, length us, event | category | flops | bytes accessed | tf_op | source)
XLA Modules:
  0.0 51.6 jit_solution(911709707988382446)
XLA Ops:
  0.6 47.3 %adafactor_step.1 = (f32[4,3,512,256]{3,2,1,0:T(8,128)S(1)}, f32[4,256,512]{2,1,0:T(8,128)S(1)}, f32[4,3,512,256]{3,2,1,0:T(8,128)S(1)}, f32[4,256,512]{2,1,0:T(...) custom-call(f32[3]{0:T(128)} %hyper.1, ...), custom_call_target="tpu_custom_call" | custom-call | tf_op jit(solution)/shard_map/adafactor_step/pallas_call | solution.py:444
  48.0 3.6 %adafactor_write.1 = (f32[4,3,512,256]{3,2,1,0:T(8,128)}, f32[4,256,512]{2,1,0:T(8,128)}, f32[3,4,512]{2,1,0:T(4,128)}, f32[3,4,256]{2,1,0:T(4,128)}, f32[4,256]{1,0:T(4,128)}, /*index=5*/f32[4,512]{1,0:T(4,128)}) custom-call(f32[4,3,512,256]{3,2,1,0:T(8,128)S(1)} %get-tuple-element.21.u_qkv, f32[4,256,512]{2,1,0:T(8,128)S(1)} %get-tuple-element.22.u_out, ...), custom_call_target="tpu_custom_call" | custom-call | tf_op jit(solution)/shard_map/adafactor_write/pallas_call | solution.py:475
